TPU v7x, 256 devices: a 2x2x32 block of a 4x8x32 slice. The times are simulated.
256 devices in a mesh: groups: 4 (over x, y), blk: 64 (over z, core).
Axes of the slice: x: 2, y: 2, z: 32, core: 2. Of those that a mesh axis runs over, the one named last changes fastest.
The devices are a block of a 4x8x32 slice.
Arguments:
- queries: bfloat16 [128, 64, 2048], P('blk', 'groups'), parts along dimension 1, may hold values from -24 to 24
- keys: bfloat16 [524288, 512], P(('groups', 'blk')), parts along dimension 0, may hold values from -24 to 24
- values: bfloat16 [524288, 512], P(('groups', 'blk')), parts along dimension 0, may hold values from -24 to 24
- out_weight: bfloat16 [2048, 2048], replicated, may hold values from -0.125 to 0.125
- chosen: int32 [64, 12], P('groups'), parts along dimension 0, may hold values from 0 to 255, as said below
- tile_start: int32 [64], P('groups'), parts along dimension 0, may hold values from 0 to 130944, as said below
Outputs:
- projected: bfloat16 [128, 64, 2048], P('blk', 'groups'), parts along dimension 1
There are 4 independent parts, one for each index of `groups`. A program takes and returns all parts, laid end to end along the dimension named above; an argument that names none is the same for every part. Nothing has to cross between parts.
Inputs may be any that keep to these rules, and one draw needn't show every extreme that they name: `chosen`: row t lists 12 different blocks; the first is the block that holds tile t's positions, the others lie before it. Each block is listed by at most 2 tiles, and some block by exactly 2. `tile_start[t]` is a multiple of 128; tile t's queries have positions tile_start[t] to tile_start[t] + 127, all inside block chosen[t, 0].
All inputs are finite; a program needn't handle non-finite values.
Results may differ from a plain program's by a relative error of at most 0.0064.
Values may be sent and summed in bfloat16 or wider, within the bound.
A program may use at most 128 MiB of HBM per device.

v0:
```python
import math
import jax
import jax.numpy as jnp
from jax import lax
from jax.sharding import PartitionSpec as P

QH = 16
KVH = 4
HD = 128
BLOCK = 512
CAP = 2
neg_big = -1e30


def visit_block(query_tile, tile_begin, block_keys, block_values, block_begin):
    tile_rows = query_tile.shape[0]
    key_count = block_keys.shape[0]
    query_view = query_tile.reshape(tile_rows, KVH, QH // KVH, HD)
    key_view = block_keys.reshape(key_count, KVH, HD)
    value_view = block_values.reshape(key_count, KVH, HD)
    scores = jnp.einsum(
        "rkgd,jkd->kgrj", query_view, key_view, preferred_element_type=jnp.float32
    ) * (1.0 / math.sqrt(HD))
    query_pos = tile_begin + jnp.arange(tile_rows, dtype=jnp.int32)
    key_pos = block_begin + jnp.arange(key_count, dtype=jnp.int32)
    visible = key_pos[None, :] <= query_pos[:, None]
    masked = jnp.where(visible, scores, neg_big)
    highest = jnp.max(masked, axis=3, keepdims=True)
    summed = jnp.sum(jnp.where(visible, jnp.exp(masked - highest), 0.0), axis=3, keepdims=True)
    log_total = highest + jnp.log(summed)
    weights = jnp.where(visible, jnp.exp(masked - log_total), 0.0).astype(jnp.bfloat16)
    partial_value = jnp.einsum(
        "kgrj,jkd->rkgd", weights, value_view, preferred_element_type=jnp.float32
    )
    partial_value = partial_value.astype(jnp.bfloat16).reshape(tile_rows, QH * HD)
    log_rows = jnp.transpose(log_total[..., 0], (2, 0, 1)).reshape(tile_rows, QH)
    return (partial_value, log_rows)


def slot_table(chosen, block_count):
    tile_count = chosen.shape[0]
    block_ids = jnp.arange(block_count, dtype=jnp.int32)
    tile_index = jnp.arange(tile_count, dtype=jnp.int32)
    member = jnp.any(chosen[None, :, :] == block_ids[:, None, None], axis=2)
    ranking = jnp.cumsum(member.astype(jnp.int32), axis=1) - 1
    slot_index = jnp.arange(CAP, dtype=jnp.int32)
    hits = member[:, None, :] & (ranking[:, None, :] == slot_index[None, :, None])
    slot_tile = jnp.sum(jnp.where(hits, tile_index[None, None, :], 0), axis=2)
    slot_live = jnp.any(hits, axis=2)
    return (hits, slot_tile, slot_live)


def on_device(queries, keys, values, out_weight, chosen, tile_start):
    owner_count = lax.axis_size("blk")
    owner_dev = lax.axis_index("blk")
    local_rows, tile_count, width = queries.shape
    per_device = keys.shape[0] // BLOCK
    slot_count = per_device * CAP
    head_count = QH
    hits_blocks, tiles_blocks, live_blocks = slot_table(chosen, owner_count * per_device)
    tiles_all = tiles_blocks.reshape(owner_count, slot_count)
    live_all = live_blocks.reshape(owner_count, slot_count)
    my_tiles = tiles_all[owner_dev]
    my_live = live_all[owner_dev]
    begins = tile_start[my_tiles]
    local_block = jnp.arange(slot_count, dtype=jnp.int32) // CAP
    gathered = lax.all_gather(queries, "blk", axis=0, tiled=True)
    slot_queries = jnp.transpose(jnp.take(gathered, my_tiles, axis=1), (1, 0, 2))

    def one_slot(inputs):
        query_tile, tile_begin, block_here = inputs
        offset = block_here * BLOCK
        block_keys = lax.dynamic_slice_in_dim(keys, offset, BLOCK, 0)
        block_values = lax.dynamic_slice_in_dim(values, offset, BLOCK, 0)
        block_begin = (owner_dev * per_device + block_here) * BLOCK
        return visit_block(query_tile, tile_begin, block_keys, block_values, block_begin)

    partials, log_slots = lax.map(one_slot, (slot_queries, begins, local_block))
    log_slots = jnp.where(my_live[:, None, None], log_slots, neg_big)
    part_out = partials.reshape(slot_count, owner_count, local_rows, width)
    peak_out = log_slots.reshape(slot_count, owner_count, local_rows, head_count)
    got_parts = lax.all_to_all(part_out, "blk", split_axis=1, concat_axis=1, tiled=True)
    got_peaks = lax.all_to_all(peak_out, "blk", split_axis=1, concat_axis=1, tiled=True)
    pair_count = slot_count * owner_count
    pair_tile = jnp.transpose(tiles_all).reshape(pair_count)
    pair_live = jnp.transpose(live_all).reshape(pair_count)
    tile_index = jnp.arange(tile_count, dtype=jnp.int32)
    pair_hits = (pair_tile[None, :] == tile_index[:, None]) & pair_live[None, :]
    peaks = got_peaks.reshape(pair_count, local_rows, head_count)
    tile_peak = jnp.max(jnp.where(pair_hits[:, :, None, None], peaks[None], neg_big), axis=1)
    pair_peak = tile_peak[pair_tile]
    factor = jnp.where(pair_live[:, None, None], jnp.exp(peaks - pair_peak), 0.0)
    weighted = factor[..., None] * got_parts.reshape(pair_count, local_rows, head_count, -1).astype(
        jnp.float32
    )
    weighted = weighted.reshape(pair_count, local_rows, width)
    pick_table = pair_hits.astype(jnp.float32)
    numer_rows = jnp.einsum("tp,prf->rtf", pick_table, weighted, precision=lax.Precision.HIGHEST)
    denom_rows = jnp.einsum("tp,prh->rth", pick_table, factor, precision=lax.Precision.HIGHEST)
    merged = numer_rows.reshape(local_rows, tile_count, head_count, -1) / denom_rows[..., None]
    merged = merged.reshape(local_rows * tile_count, width).astype(jnp.bfloat16)
    result = jnp.dot(merged, out_weight, preferred_element_type=jnp.float32).astype(jnp.bfloat16)
    return result.reshape(local_rows, tile_count, out_weight.shape[1])


def solution(mesh):
    placed = (
        P("blk", "groups", None),
        P(("groups", "blk"), None),
        P(("groups", "blk"), None),
        P(),
        P("groups", None),
        P("groups"),
    )
    return jax.shard_map(
        on_device, mesh=mesh, in_specs=placed, out_specs=P("blk", "groups", None), check_vma=False
    )
```

profile of v0, /device:TPU:38, one launch (start us, length us, event | category | flops | bytes accessed | tf_op | source)
XLA Modules:
  0.0 728.5 jit_solution(17762847718979088911)
XLA Ops:
  9.6 149.9 %all-gather.2.cloned.1.call-done = bf16[128,16,2048]{2,1,0:T(8,128)(2,1)} async-done(((bf16[2,16,2048]{2,1,0:T(8,128)(2,1)}), bf16[128,16,2048]{2,1,0:T(8,128)(2,1)}) %all-gather.2.cloned.1.call-update) | async-done | bytes 8388624 | tf_op jit(solution)/shard_map/all_gather | solution.py:67
  159.5 11.2 %copy.79 = bf16[128,16,2048]{2,0,1:T(8,128)(2,1)} copy(bf16[128,16,2048]{2,1,0:T(8,128)(2,1)} %all-gather.2.cloned.1.call-done) | data formatting | bytes 16777216 | tf_op jit(solution)/shard_map/all_gather | solution.py:67
  170.7 6.1 gather_fusion.1
  176.9 4.6 broadcast_select_fusion
  181.4 81.9 %while.14 = (s32[]{:T(128)}, bf16[8,128,2048]{1,2,0:T(8,128)(2,1)}, f32[8,128,16]{1,2,0:T(8,128)S(1)}, s32[8]{0:T(128)S(1)}, bf16[2048,512]{1,0:T(8,128)(2,1)}, ...) while((s32[]{:T(128)}, bf16[8,128,2048]{1,2,0:T(8,128)(2,1)}, ...), condition=%wide.region_7.8_spmd, body=%wide.region_4.7_spmd.sunk | while | flops 550828672 | bytes 22361340 | solution.py:78
  182.7 1.3 constant_dynamic-slice_fusion.6
  186.4 1.1 constant_dynamic-slice_fusion.7
  188.6 1.0 select_reduce_fusion.4
  189.6 1.2 fusion.34
  192.9 1.3 constant_dynamic-slice_fusion.6
  196.6 1.1 constant_dynamic-slice_fusion.7
  198.8 1.0 select_reduce_fusion.4
  199.8 1.2 fusion.34
  203.1 1.3 constant_dynamic-slice_fusion.6
  206.8 1.1 constant_dynamic-slice_fusion.7
  209.0 1.0 select_reduce_fusion.4
  210.1 1.2 fusion.34
  213.4 1.3 constant_dynamic-slice_fusion.6
  217.1 1.1 constant_dynamic-slice_fusion.7
  219.3 1.0 select_reduce_fusion.4
  220.3 1.2 fusion.34
  223.6 1.3 constant_dynamic-slice_fusion.6
  227.3 1.1 constant_dynamic-slice_fusion.7
  229.5 1.0 select_reduce_fusion.4
  230.6 1.2 fusion.34
  233.8 1.3 constant_dynamic-slice_fusion.6
  237.5 1.1 constant_dynamic-slice_fusion.7
  239.7 1.0 select_reduce_fusion.4
  240.8 1.2 fusion.34
  244.1 1.3 constant_dynamic-slice_fusion.6
  247.8 1.1 constant_dynamic-slice_fusion.7
  251.0 1.2 fusion.34
  254.3 1.3 constant_dynamic-slice_fusion.6
  258.0 1.1 constant_dynamic-slice_fusion.7
  261.3 1.2 fusion.34
  264.5 14.5 %all-to-all-start = ((f32[64,1,256]{2,1,0:T(1,128)}), f32[64,1,256]{2,1,0:T(1,128)S(1)}, u32[]{:S(2)}, u32[]{:S(2)}) async-start(f32[64,1,256]{2,1,0:T(1,128)} %reshape.230), calls=%async_computation | async-start | bytes 131072 | tf_op jit(solution)/shard_map/all_to_all | solution.py:83
  279.0 6.7 copy.89
  285.7 18.1 %all-to-all-done = f32[64,1,256]{2,1,0:T(1,128)S(1)} async-done(((f32[64,1,256]{2,1,0:T(1,128)}), f32[64,1,256]{2,1,0:T(1,128)S(1)}, u32[]{:S(2)}, u32[]{:S(2)}) %all-to-all-start) | async-done | bytes 65568 | tf_op jit(solution)/shard_map/all_to_all | solution.py:83
  303.9 7.3 %all-to-all-start.1 = ((bf16[8,64,2,2048]{3,0,2,1:T(8,128)(2,1)}), bf16[8,64,2,2048]{3,0,2,1:T(8,128)(2,1)}, u32[]{:S(2)}, u32[]{:S(2)}) async-start(bf16[8,64,2,2048]{3,0,2,1:T(8,128)(2,1)} %bitcast.114), calls=%async_computation.1 | async-start | bytes 8388608 | tf_op jit(solution)/shard_map/all_to_all | solution.py:82
  313.8 2.1 gather_fusion.2
  315.9 1.8 exponential_select_fusion
  318.3 5.1 mul.35
  323.4 9.3 %mul.36 = f32[512,2,2048]{2,0,1:T(8,128)} reshape(f32[512,2,16,128]{3,2,0,1:T(8,128)} %mul.35) | data formatting | bytes 16777216 | tf_op jit(solution)/shard_map/mul | solution.py:93
  332.7 357.4 %all-to-all-done.1 = bf16[8,64,2,2048]{3,0,2,1:T(8,128)(2,1)} async-done(((bf16[8,64,2,2048]{3,0,2,1:T(8,128)(2,1)}), bf16[8,64,2,2048]{3,0,2,1:T(8,128)(2,1)}, u32[]{:S(2)}, u32[]{:S(2)}) %all-to-all-start.1) | async-done | bytes 4194336 | tf_op jit(solution)/shard_map/all_to_all | solution.py:82
  690.1 7.8 %copy.90 = f32[8,64,2,2048]{3,1,0,2:T(8,128)} copy(bf16[8,64,2,2048]{3,0,2,1:T(8,128)(2,1)} %all-to-all-done.1) | data formatting | bytes 12582912 | tf_op jit(solution)/shard_map/convert_element_type | solution.py:93
  697.9 11.7 %bitcast_multiply_fusion = f32[512,2,2048]{2,0,1:T(8,128)} fusion(f32[512,2,2048]{2,0,1:T(8,128)} %mul.36, f32[8,64,2,2048]{3,1,0,2:T(8,128)} %copy.90), kind=kLoop, calls=%fused_computation.22 | loop fusion | flops 2097152 | bytes 25165824 | tf_op jit(solution)/shard_map/mul | solution.py:93
  709.6 6.1 fusion.13
  716.0 5.6 convolution_convert_fusion
  (145 shorter events, 44.3 us)
Async XLA Ops:
  6.5 2.4 copy-start
  6.6 153.0 %all-gather.2.cloned.1.call-start = ((), (), s32[]{:S(2)}) async-start(), calls=%async_computation.2 | async-start | bytes 8519680 | tf_op jit(solution)/shard_map/all_gather | solution.py:67
  264.5 39.4 %all-to-all-start = ((f32[64,1,256]{2,1,0:T(1,128)}), f32[64,1,256]{2,1,0:T(1,128)S(1)}, u32[]{:S(2)}, u32[]{:S(2)}) async-start(f32[64,1,256]{2,1,0:T(1,128)} %reshape.230), calls=%async_computation | async-start | bytes 131072 | tf_op jit(solution)/shard_map/all_to_all | solution.py:83
  303.9 386.3 %all-to-all-start.1 = ((bf16[8,64,2,2048]{3,0,2,1:T(8,128)(2,1)}), bf16[8,64,2,2048]{3,0,2,1:T(8,128)(2,1)}, u32[]{:S(2)}, u32[]{:S(2)}) async-start(bf16[8,64,2,2048]{3,0,2,1:T(8,128)(2,1)} %bitcast.114), calls=%async_computation.1 | async-start | bytes 8388608 | tf_op jit(solution)/shard_map/all_to_all | solution.py:82
  715.9 5.7 copy-start.1
Sparse Core Ops, SparseCore 0:
  9.2 150.2 all-gather.1
where the time goes:
time: 730 us; the launch traced here: 728 us
  waiting for transfers between devices  526 us (72%)
  local copies, waits for them, and re-layouts  94.1 us (13%)
  other arithmetic  33.9 us (5%)
  matrix products  28.4 us (4%)
  starting transfers between devices  21.8 us (3%)
  between operations  13.6 us (2%)
  loops' own time  10.4 us (1%)
    all_to_all x1, waiting for transfers between devices, on_device(): lax.all_to_all(part_out, 'blk', split_axis=1, concat_axis=1, tiled=True)  357 us
    all_gather x1, waiting for transfers between devices, on_device(): gathered = lax.all_gather(queries, 'blk', axis=0, tiled=True)  150 us
    dynamic_slice x32, local copies, waits for them, and re-layouts, on_device(): partials, log_slots = lax.map(one_slot, (slot_queries, begins, local_block))  20.5 us
    all_to_all x1, waiting for transfers between devices, on_device(): lax.all_to_all(peak_out, 'blk', split_axis=1, concat_axis=1, tiled=True)  18.1 us
  transfers between devices with their start and end apart: 3, of which 3 were waited for; matrix products, arithmetic and copies ran while one was open for 4% of the time, Pallas kernels for 0%

commit v1 on v0

--- a/solution.py
+++ b/solution.py
@@ -10,6 +10,10 @@
 BLOCK = 512
 CAP = 2
 neg_big = -1e30
+perform_roads = lambda original, mesh_name: jnp.concatenate(
+    lax.all_to_all(jnp.stack([original for _ in range(lax.axis_size(mesh_name))]), mesh_name, 0, 0),
+    axis=0,
+)
 
 
 def visit_block(query_tile, tile_begin, block_keys, block_values, block_begin):
@@ -64,7 +68,7 @@
     my_live = live_all[owner_dev]
     begins = tile_start[my_tiles]
     local_block = jnp.arange(slot_count, dtype=jnp.int32) // CAP
-    gathered = lax.all_gather(queries, "blk", axis=0, tiled=True)
+    gathered = perform_roads(queries, "blk")
     slot_queries = jnp.transpose(jnp.take(gathered, my_tiles, axis=1), (1, 0, 2))
 
     def one_slot(inputs):

time: 730 us -> 1350 us (1.85)
  waiting for transfers between devices: 526 us -> 1110 us
  starting transfers between devices: 21.8 us -> 48.3 us
  local copies, waits for them, and re-layouts: 94.1 us -> 110 us
    all_to_all x0 -> x1, waiting for transfers between devices: none -> 737 us  [lax.all_to_all(jnp.stack([original for _ in range(lax.axis_size(mesh_name...]
    all_gather x1 -> x0, waiting for transfers between devices: 150 us -> none  [on_device(): gathered = lax.all_gather(queries, 'blk', axis=0, tiled=True)]
    all_to_all x0 -> x1, starting transfers between devices: none -> 34.4 us  [lax.all_to_all(jnp.stack([original for _ in range(lax.axis_size(mesh_name...]
  transfers between devices with their start and end apart: 3 -> 3, of which waited for: 3 -> 3; matrix products, arithmetic and copies ran while one was open for 4% -> 2% of each run, Pallas kernels for 0% -> 0%
where the time goes in v1:
time: 1350 us; the launch traced here: 1340 us
  waiting for transfers between devices  1110 us (82%)
  local copies, waits for them, and re-layouts  110 us (8%)
  starting transfers between devices  48.3 us (4%)
  other arithmetic  34.5 us (3%)
  matrix products  28.4 us (2%)
    all_to_all x1, waiting for transfers between devices, lax.all_to_all(jnp.stack([original for _ in range(lax.axis_size(mesh_name...  737 us
    all_to_all x1, waiting for transfers between devices, on_device(): lax.all_to_all(part_out, 'blk', split_axis=1, concat_axis=1, tiled=True)  357 us
    all_to_all x1, starting transfers between devices, lax.all_to_all(jnp.stack([original for _ in range(lax.axis_size(mesh_name...  34.4 us
  transfers between devices with their start and end apart: 3, of which 3 were waited for; matrix products, arithmetic and copies ran while one was open for 2% of the time, Pallas kernels for 0%

profile of v1, /device:TPU:38, one launch (start us, length us, event | category | flops | bytes accessed | tf_op | source)
XLA Modules:
  0.0 1344.3 jit_solution(7931290062621199775)
XLA Ops:
  0.0 1.1 copy.80
  1.1 5.6 stack.2
  6.7 34.4 %all-to-all-start = ((bf16[64,2,16,2048]{3,1,2,0:T(2,128)(2,1)}), bf16[64,2,16,2048]{3,1,2,0:T(2,128)(2,1)}, u32[]{:S(2)}, u32[]{:S(2)}) async-start(bf16[64,2,16,2048]{3,1,2,0:T(2,128)(2,1)} %stack.2), calls=%async_computation | async-start | bytes 16777216 | tf_op jit(solution)/shard_map/all_to_all | solution.py:14
  42.7 736.8 %all-to-all-done = bf16[64,2,16,2048]{3,1,2,0:T(2,128)(2,1)} async-done(((bf16[64,2,16,2048]{3,1,2,0:T(2,128)(2,1)}), bf16[64,2,16,2048]{3,1,2,0:T(2,128)(2,1)}, u32[]{:S(2)}, u32[]{:S(2)}) %all-to-all-start) | async-done | bytes 8388640 | tf_op jit(solution)/shard_map/all_to_all | solution.py:14
  779.5 8.0 copy.81
  787.4 13.1 reshape.201
  800.5 6.2 gather_fusion.1
  806.7 4.6 broadcast_select_fusion
  811.3 82.7 %while.14 = (s32[]{:T(128)}, bf16[8,128,2048]{1,2,0:T(8,128)(2,1)}, f32[8,128,16]{1,2,0:T(8,128)S(1)}, s32[8]{0:T(128)S(1)}, bf16[2048,512]{1,0:T(8,128)(2,1)}, ...) while((s32[]{:T(128)}, bf16[8,128,2048]{1,2,0:T(8,128)(2,1)}, ...), condition=%wide.region_7.8_spmd, body=%wide.region_4.7_spmd.sunk | while | flops 550828672 | bytes 22361340 | solution.py:82
  812.6 1.3 constant_dynamic-slice_fusion.6
  816.4 1.1 constant_dynamic-slice_fusion.7
  818.6 1.0 select_reduce_fusion.4
  819.6 1.2 fusion.34
  822.9 1.3 constant_dynamic-slice_fusion.6
  826.7 1.1 constant_dynamic-slice_fusion.7
  828.9 1.0 select_reduce_fusion.4
  829.9 1.2 fusion.34
  833.2 1.3 constant_dynamic-slice_fusion.6
  837.0 1.1 constant_dynamic-slice_fusion.7
  840.3 1.2 fusion.34
  843.6 1.3 constant_dynamic-slice_fusion.6
  847.4 1.1 constant_dynamic-slice_fusion.7
  850.6 1.2 fusion.34
  853.9 1.3 constant_dynamic-slice_fusion.6
  857.7 1.1 constant_dynamic-slice_fusion.7
  861.0 1.2 fusion.34
  864.2 1.3 constant_dynamic-slice_fusion.6
  868.0 1.1 constant_dynamic-slice_fusion.7
  871.3 1.2 fusion.34
  874.6 1.3 constant_dynamic-slice_fusion.6
  878.4 1.1 constant_dynamic-slice_fusion.7
  881.6 1.2 fusion.34
  884.9 1.3 constant_dynamic-slice_fusion.6
  888.7 1.1 constant_dynamic-slice_fusion.7
  891.9 1.2 fusion.34
  895.2 6.5 all-to-all-start.1
  901.7 6.7 copy.91
  908.4 18.1 %all-to-all-done.1 = f32[64,1,256]{2,1,0:T(1,128)S(1)} async-done(((f32[64,1,256]{2,1,0:T(1,128)}), f32[64,1,256]{2,1,0:T(1,128)S(1)}, u32[]{:S(2)}, u32[]{:S(2)}) %all-to-all-start.1) | async-done | bytes 65568 | tf_op jit(solution)/shard_map/all_to_all | solution.py:87
  926.5 7.5 all-to-all-start.2
  936.6 2.1 gather_fusion.2
  938.7 1.8 exponential_select_fusion
  941.1 5.1 mul.35
  946.3 9.3 mul.36
  955.5 357.2 %all-to-all-done.2 = bf16[8,64,2,2048]{3,0,2,1:T(8,128)(2,1)} async-done(((bf16[8,64,2,2048]{3,0,2,1:T(8,128)(2,1)}), bf16[8,64,2,2048]{3,0,2,1:T(8,128)(2,1)}, u32[]{:S(2)}, u32[]{:S(2)}) %all-to-all-start.2) | async-done | bytes 4194336 | tf_op jit(solution)/shard_map/all_to_all | solution.py:86
  1312.8 7.8 copy.92
  1320.6 11.7 bitcast_multiply_fusion
  1332.3 6.1 fusion.13
  1338.7 5.6 convolution_convert_fusion
  (149 shorter events, 48.1 us)
Async XLA Ops:
  0.0 42.0 %copy-start = (s32[16]{0:T(128)S(1)}, s32[16]{0:T(128)}, u32[]{:S(2)}) copy-start(s32[16]{0:T(128)} %param.13) | copy-start | bytes 196
  6.7 34.4 %copy-start.2 = (s32[16,12]{1,0:T(8,128)S(1)}, s32[16,12]{1,0:T(8,128)}, u32[]{:S(2)}) copy-start(s32[16,12]{1,0:T(8,128)} %param.12) | copy-start | bytes 2308
  6.7 772.8 %all-to-all-start = ((bf16[64,2,16,2048]{3,1,2,0:T(2,128)(2,1)}), bf16[64,2,16,2048]{3,1,2,0:T(2,128)(2,1)}, u32[]{:S(2)}, u32[]{:S(2)}) async-start(bf16[64,2,16,2048]{3,1,2,0:T(2,128)(2,1)} %stack.2), calls=%async_computation | async-start | bytes 16777216 | tf_op jit(solution)/shard_map/all_to_all | solution.py:14
  895.2 31.3 %all-to-all-start.1 = ((f32[64,1,256]{2,1,0:T(1,128)}), f32[64,1,256]{2,1,0:T(1,128)S(1)}, u32[]{:S(2)}, u32[]{:S(2)}) async-start(f32[64,1,256]{2,1,0:T(1,128)} %reshape.236), calls=%async_computation.1 | async-start | bytes 131072 | tf_op jit(solution)/shard_map/all_to_all | solution.py:87
  926.5 386.3 %all-to-all-start.2 = ((bf16[8,64,2,2048]{3,0,2,1:T(8,128)(2,1)}), bf16[8,64,2,2048]{3,0,2,1:T(8,128)(2,1)}, u32[]{:S(2)}, u32[]{:S(2)}) async-start(bf16[8,64,2,2048]{3,0,2,1:T(8,128)(2,1)} %bitcast.116), calls=%async_computation.2 | async-start | bytes 8388608 | tf_op jit(solution)/shard_map/all_to_all | solution.py:86
  1338.5 5.7 copy-start.1
